TPU v7x, 32 devices: a whole 2x2x4 slice. The times are simulated.
32 devices in a mesh: seq: 8 (over z, y), grp: 4 (over x, core).
Axes of the slice: x: 2, y: 2, z: 4, core: 2. Of those that a mesh axis runs over, the one named last changes fastest.
Arguments:
- hidden: bfloat16 [256, 8192], P('grp', 'seq'), may hold values from -6 to 6
- w_qkv: bfloat16 [8192, 10240], P('seq', 'grp'), may hold values from -0.0625 to 0.0625
- b_qkv: float32 [10240], P('grp'), may hold values from -3 to 3
- w_out: bfloat16 [8192, 8192], P('seq', 'grp'), may hold values from -0.0625 to 0.0625
- k_cache: bfloat16 [4, 32768, 1024], P('grp', 'seq'), may hold values from -600 to 600
- v_cache: bfloat16 [4, 32768, 1024], P('grp', 'seq'), may hold values from -6 to 6
- lengths: int32 [256], replicated, may hold values from 1 to 16384, as said below
- page_table: int32 [256, 128], replicated, may hold values from -1 to 255, as said below
- positions: int32 [3, 256], replicated, may hold values from 0 to 4095
- group_of: int32 [256], replicated, may hold values from 0 to 3, as said below
Outputs:
- mixed: bfloat16 [256, 8192], P('seq', 'grp')
Inputs may be any that keep to these rules, and one draw needn't show every extreme that they name: `group_of`: each group serves exactly 64 requests. `lengths`: each group has a request of exactly 16384 cached positions. `page_table`: entry j of row r is the page of request r's group pool (page p lies on that group's device p // 32 of seq) that holds its positions j * 128 to (j + 1) * 128 - 1, for j < ceil(lengths[r] / 128); later entries are -1; no page belongs to two requests.
All inputs are finite; a program needn't handle non-finite values.
Results may differ from a plain program's by a relative error of at most 0.015.
The roundings to bfloat16 on the way count: a program that leaves them out, or rounds other values in their place, can miss the bound.
Values may be sent and summed in bfloat16 or wider, within the bound.
A program may use at most 128 MiB of HBM per device.

v0:
```python
import math
import jax
import jax.numpy as jnp
from jax import lax
from jax.sharding import PartitionSpec as P

HQ = 64
KVH = 8
HD = 128
PAGE = 128
rope_base = 1000000.0
neg_fill = -1e30


def rotate_heads(values, places, col_start, head_dim, turned):
    row_count, col_count = values.shape
    columns = col_start + jnp.arange(col_count, dtype=jnp.int32)
    within = columns % head_dim
    freq_index = within % (head_dim // 2)
    inverse_freq = jnp.exp(freq_index.astype(jnp.float32) * (-2.0 * math.log(rope_base) / head_dim))
    section = jnp.where(
        freq_index < head_dim // 8,
        0,
        jnp.where(freq_index < head_dim // 8 + 3 * head_dim // 16, 1, 2),
    )
    place_float = places.astype(jnp.float32)
    chosen = jnp.where(
        section[None, :] == 0,
        place_float[0][:, None],
        jnp.where(section[None, :] == 1, place_float[1][:, None], place_float[2][:, None]),
    )
    angles = chosen * inverse_freq[None, :]
    halves = values.reshape(row_count, col_count // head_dim, 2, head_dim // 2)
    partner = jnp.concatenate([-halves[:, :, 1:], halves[:, :, :1]], axis=2).reshape(
        row_count, col_count
    )
    rotated = values * jnp.cos(angles) + partner * jnp.sin(angles)
    return jnp.where((columns < turned)[None, :], rotated, values)


def shards(hidden, w_qkv, b_qkv, w_out, k_cache, v_cache, lengths, page_table, positions, group_of):
    seq_count = lax.axis_size("seq")
    grp_count = lax.axis_size("grp")
    seq_index = lax.axis_index("seq")
    grp_index = lax.axis_index("grp")
    request_total = group_of.shape[0]
    group_size = request_total // grp_count
    col_count = w_qkv.shape[1]
    col_start = grp_index * col_count
    turned = (HQ + KVH) * HD
    group_q = HQ // KVH
    score_scale = HD ** (-0.5)
    partial_sum = jnp.dot(
        lax.all_gather(hidden, "grp", axis=0, tiled=True), w_qkv, preferred_element_type=jnp.float32
    )
    request_ids = jnp.arange(request_total, dtype=jnp.int32)
    before = (group_of[None, :] < group_of[:, None]) | (group_of[None, :] == group_of[:, None]) & (
        request_ids[None, :] < request_ids[:, None]
    )
    restore = jnp.sum(before.astype(jnp.int32), axis=1)
    placed_at = restore[None, :] == request_ids[:, None]
    served_order = jnp.sum(jnp.where(placed_at, request_ids[None, :], 0), axis=1)
    served_ids = lax.dynamic_slice_in_dim(served_order, grp_index * group_size, group_size, 0)
    summed = lax.psum(partial_sum, "seq")
    fresh_rows = rotate_heads(summed + b_qkv[None, :], positions, col_start, HD, turned).astype(
        jnp.bfloat16
    )
    outgoing = fresh_rows[served_order].reshape(grp_count, group_size, col_count)
    incoming = lax.all_to_all(outgoing, "grp", split_axis=0, concat_axis=2, tiled=True)
    served_rows = incoming.reshape(group_size, grp_count * col_count)
    query_rows = served_rows[:, : HQ * HD]
    key_new = served_rows[:, HQ * HD : turned]
    value_new = served_rows[:, turned:]
    served_len = lengths[served_ids]
    served_table = page_table[served_ids]
    most_pages = page_table.shape[1]
    page_counts = (served_len + PAGE - 1) // PAGE
    logical = jnp.arange(most_pages, dtype=jnp.int32)
    pool_pages = k_cache.shape[1] // PAGE
    local_page = served_table - seq_index * pool_pages
    usable = (
        (logical[None, :] < page_counts[:, None]) & (local_page >= 0) & (local_page < pool_pages)
    )
    pool_ids = jnp.arange(pool_pages, dtype=jnp.int32)
    matched = usable[:, :, None] & (local_page[:, :, None] == pool_ids[None, None, :])
    owner_ids = jnp.arange(group_size, dtype=jnp.int32)
    page_owner = jnp.max(jnp.where(matched, owner_ids[:, None, None], -1), axis=(0, 1))
    page_number = jnp.max(jnp.where(matched, logical[None, :, None], 0), axis=(0, 1))
    present = page_owner >= 0
    holder = jnp.maximum(page_owner, 0)
    page_query = query_rows[holder].reshape(pool_pages, KVH, group_q, HD)
    page_keys = k_cache[0].reshape(pool_pages, PAGE, KVH, HD)
    page_values = v_cache[0].reshape(pool_pages, PAGE, KVH, HD)
    scores = (
        jnp.einsum("pkgd,ptkd->pkgt", page_query, page_keys, preferred_element_type=jnp.float32)
        * score_scale
    )
    places_in = page_number[:, None] * PAGE + jnp.arange(PAGE, dtype=jnp.int32)[None, :]
    alive_rows = present[:, None] & (places_in < served_len[holder][:, None])
    alive_wide = alive_rows[:, None, None, :]
    page_max = jnp.max(jnp.where(alive_wide, scores, neg_fill), axis=3)
    weights = jnp.exp(jnp.where(alive_wide, scores - page_max[..., None], neg_fill))
    page_total = jnp.sum(weights, axis=3).reshape(pool_pages, HQ)
    page_out = jnp.einsum(
        "pkgt,ptkd->pkgd",
        weights.astype(jnp.bfloat16),
        page_values,
        preferred_element_type=jnp.float32,
    ).reshape(pool_pages, HQ, HD)
    page_max = page_max.reshape(pool_pages, HQ)
    member = page_owner[:, None] == owner_ids[None, :]
    local_max = jnp.max(jnp.where(member[:, :, None], page_max[:, None, :], neg_fill), axis=0)
    factor = jnp.where(present[:, None], jnp.exp(page_max - local_max[holder]), 0.0)
    member_float = member.astype(jnp.float32)
    local_total = jnp.einsum(
        "pr,ph->rh", member_float, page_total * factor, precision=lax.Precision.HIGHEST
    )
    local_out = jnp.einsum(
        "pr,pe->re",
        member_float,
        (page_out * factor[..., None]).reshape(pool_pages, HQ * HD),
        precision=lax.Precision.HIGHEST,
    )
    new_score = (
        jnp.einsum(
            "rkgd,rkd->rkg",
            query_rows.reshape(group_size, KVH, group_q, HD),
            key_new.reshape(group_size, KVH, HD),
            preferred_element_type=jnp.float32,
        ).reshape(group_size, HQ)
        * score_scale
    )
    head_share = HQ // seq_count
    head_start = seq_index * head_share
    value_heads = jnp.broadcast_to(
        value_new.reshape(group_size, KVH, 1, HD), (group_size, KVH, group_q, HD)
    ).reshape(group_size, HQ, HD)
    value_here = lax.dynamic_slice_in_dim(value_heads, head_start, head_share, 1).astype(
        jnp.float32
    )
    new_here = lax.dynamic_slice_in_dim(new_score, head_start, head_share, 1)
    peak_score = lax.pmax(jnp.maximum(local_max, new_score), "seq")
    kept_scale = jnp.exp(local_max - peak_score)
    scaled_out = (local_out.reshape(group_size, HQ, HD) * kept_scale[..., None]).reshape(
        group_size, HQ * HD
    )
    shared_out, shared_total = (
        lax.psum_scatter(scaled_out, "seq", scatter_dimension=1, tiled=True),
        lax.psum_scatter(local_total * kept_scale, "seq", scatter_dimension=1, tiled=True),
    )
    peak_here = lax.dynamic_slice_in_dim(peak_score, head_start, head_share, 1)
    fresh_weight = jnp.exp(new_here - peak_here)
    denominator = shared_total + fresh_weight
    numerator = (
        shared_out.reshape(group_size, head_share, HD) + fresh_weight[..., None] * value_here
    )
    attended = (
        (numerator / denominator[..., None])
        .reshape(group_size, head_share * HD)
        .astype(jnp.bfloat16)
    )
    gathered = lax.all_gather(attended, "grp", axis=0, tiled=True)
    by_request = gathered[restore]
    return lax.psum_scatter(
        jnp.dot(by_request, w_out, preferred_element_type=jnp.float32).astype(jnp.bfloat16),
        "seq",
        scatter_dimension=0,
        tiled=True,
    )


def solution(mesh):
    placed = (
        P("grp", "seq"),
        P("seq", "grp"),
        P("grp"),
        P("seq", "grp"),
        P("grp", "seq", None),
        P("grp", "seq", None),
        P(),
        P(),
        P(),
        P(),
    )
    return jax.shard_map(
        shards, mesh=mesh, in_specs=placed, out_specs=P("seq", "grp"), check_vma=False
    )
```

profile of v0, /device:TPU:0, one launch (start us, length us, event | category | flops | bytes accessed | tf_op | source)
XLA Modules:
  0.0 401.6 jit_solution(12910051012480212838)
XLA Ops:
  6.5 9.0 %all_gather.6 = bf16[256,1024]{1,0:T(8,128)(2,1)S(1)} all-gather(bf16[64,1024]{1,0:T(8,128)(2,1)} %param.10), channel_id=1, replica_groups=mesh['seq'=8,'grp'=4] {'grp'}, dimensions={0}, use_global_device_ids=true | all-gather | bytes 655360 | tf_op jit(solution)/shard_map/all_gather | solution.py:54
  15.5 5.5 %fusion.40 = f32[256,2560]{1,0:T(8,128)} fusion(bf16[256,1024]{1,0:T(8,128)(2,1)S(1)} %all_gather.6, bf16[1024,2560]{1,0:T(8,128)(2,1)} %param.11), kind=kOutput, calls=%fused_computation.102 | convolution fusion | flops 1342177280 | bytes 8388608 | tf_op jit(solution)/shard_map/dot_general | solution.py:53
  21.1 0.6 copy-done.12
  22.1 0.8 gather_fusion
  22.9 0.6 gather_fusion.1
  23.5 0.6 compare_select_fusion
  24.3 0.6 select_reduce_fusion.2
  24.9 113.1 %all-reduce.3.cloned.1.call-done = f32[256,2560]{1,0:T(8,128)} async-done(((f32[256,2560]{1,0:T(8,128)}), f32[256,2560]{1,0:T(8,128)}) %all-reduce.3.cloned.1.call-update) | async-done | bytes 2621456 | tf_op jit(solution)/shard_map/psum | solution.py:64
  138.0 3.6 broadcast_add_fusion
  141.6 2.1 copy.46
  144.1 2.1 copy.47
  146.2 11.8 %select_convert_fusion = bf16[256,2560]{1,0:T(8,128)(2,1)S(1)} fusion(f32[256,2560]{1,0:T(8,128)} %copy.47, f32[2560]{0:T(1024)S(1)} %multiply_exponential_fusion, f32[256]{0:T(256)S(1)} %bitcast.123, f32[256]{0:T(256)S(1)} %bitcast.124, f32[256]{0:T(256)S(1)} %bitcast.122, pred[2560]{0:T(1024)(128)(4,1)S(1)} %get-tuple-element.26, ...), kind=kLoop, calls=%fused_computation.12 | loop fusion | flops 5898240 | bytes 6584832 | tf_op jit(solution)/shard_map/convert_element_type | solution.py:65
  158.0 2.5 gather_fusion.3
  160.5 3.5 all-to-all-start
  164.4 0.7 gather_fusion.2
  165.1 8.8 %copy.68 = bf16[512,8,8,128]{3,2,1,0:T(8,128)(2,1)} copy(bf16[512,8,8,128]{3,1,2,0:T(8,128)(2,1)} %bitcast.100) | data formatting | bytes 16777216
  173.8 8.8 %copy.69 = bf16[512,8,8,128]{3,2,1,0:T(8,128)(2,1)} copy(bf16[512,8,8,128]{3,1,2,0:T(8,128)(2,1)} %bitcast.101) | data formatting | bytes 16777216
  182.6 0.7 iota_compare_fusion.4
  183.4 1.0 copy.48
  184.6 0.3 slice_bitcast_fusion.1
  184.9 1.7 gather_fusion.4
  186.6 1.2 copy.67
  187.8 6.9 %select_reduce_fusion.1 = (f32[32,8,8]{2,1,0:T(8,128)S(1)}, f32[32,8,8,128]{3,2,1,0:T(8,128)S(1)}) fusion(pred[32,128]{1,0:T(8,128)(4,1)S(1)} %fusion.25, bf16[32,8,8,128]{3,2,1,0:T(8,128)(2,1)S(1)} %bitcast.109, bf16[32,128,8,128]{3,2,1,0:T(8,128)(2,1)} %bitcast.97), kind=kOutput, calls=%fused_computation.26 | convolution fusion | flops 67893248 | bytes 9973760 | tf_op jit(solution)/shard_map/pkgd,ptkd->pkgt/dot_general | solution.py:95
  194.7 0.7 copy.51
  195.4 0.8 copy.53
  196.3 1.6 select_reduce_fusion
  197.9 2.0 gather_fusion.5
  199.9 1.4 copy.56
  201.4 0.7 slice_bitcast_fusion
  202.1 1.4 exponential_select_fusion
  203.5 0.3 copy.72
  203.8 1.0 reshape.359
  204.8 0.7 fusion.41
  205.6 35.0 %pmax.7 = f32[64,64]{0,1:T(8,128)S(1)} all-reduce(f32[64,64]{0,1:T(8,128)S(1)} %fusion.38), channel_id=1, replica_groups=mesh['seq'=8,'grp'=4] {'seq'}, use_global_device_ids=true, to_apply=%region_7.8 | all-reduce | flops 4096 | bytes 32768 | tf_op jit(solution)/shard_map/pmax | solution.py:142
  240.7 6.1 %fusion = f32[32,8,8,128]{3,2,1,0:T(8,128)S(1)} fusion(bf16[32,128,8,128]{3,2,1,0:T(8,128)(2,1)} %bitcast.96, f32[32,8,8,128]{3,2,1,0:T(8,128)S(1)} %get-tuple-element.21, f32[32,8,8]{2,1,0:T(8,128)S(1)} %get-tuple-element.20, pred[32,128]{1,0:T(8,128)(4,1)S(1)} %copy-done.6), kind=kOutput, calls=%fused_computation.7 | convolution fusion | flops 67895296 | bytes 10498048 | tf_op jit(solution)/shard_map/pkgt,ptkd->pkgd/dot_general | solution.py:104
  246.7 0.3 mul.108
  247.1 2.5 multiply_bitcast_fusion
  249.6 1.5 copy.96
  251.2 0.7 dynamic-slice
  252.5 0.7 fusion.11
  253.6 33.8 %all-reduce = f32[64,64]{0,1:T(8,128)S(1)} all-reduce(f32[64,64]{0,1:T(8,128)S(1)} %convolution_multiply_fusion), channel_id=3, replica_groups=mesh['seq'=8,'grp'=4] {'seq'}, use_global_device_ids=true, to_apply=%region_10.11.clone | all-reduce | flops 4096 | bytes 32768
  287.7 0.3 broadcast_bitcast_fusion
  288.0 29.7 %reduce-scatter.3.cloned.1.call-done = f32[64,1024]{1,0:T(8,128)} async-done(((f32[64,8192]{1,0:T(8,128)}), f32[64,1024]{1,0:T(8,128)}) %reduce-scatter.3.cloned.1.call-update) | async-done | bytes 262160 | tf_op jit(solution)/shard_map/reduce_scatter | solution.py:148
  317.7 1.0 copy.73
  318.9 7.2 %all_gather.7 = bf16[256,1024]{1,0:T(8,128)(2,1)S(1)} all-gather(bf16[64,1024]{1,0:T(8,128)(2,1)S(1)} %bitcast.113), channel_id=1, replica_groups=mesh['seq'=8,'grp'=4] {'grp'}, dimensions={0}, use_global_device_ids=true | all-gather | bytes 655360 | tf_op jit(solution)/shard_map/all_gather | solution.py:162
  326.1 1.2 gather_fusion.6
  327.3 4.4 %convolution_convert_fusion = bf16[256,2048]{1,0:T(8,128)(2,1)} fusion(bf16[256,1024]{1,0:T(8,128)(2,1)S(1)} %gather_fusion.6, bf16[1024,2048]{1,0:T(8,128)(2,1)} %param.13), kind=kOutput, calls=%fused_computation.13 | convolution fusion | flops 1074266112 | bytes 5767168 | tf_op jit(solution)/shard_map/dot_general | solution.py:165
  331.7 63.4 %reduce-scatter.5.cloned.1.call-done = bf16[32,2048]{1,0:T(8,128)(2,1)} async-done(((bf16[256,2048]{1,0:T(8,128)(2,1)}), bf16[32,2048]{1,0:T(8,128)(2,1)}) %reduce-scatter.5.cloned.1.call-update) | async-done | bytes 131088 | tf_op jit(solution)/shard_map/reduce_scatter | solution.py:164
  (73 shorter events, 2.7 us)
Async XLA Ops:
  6.5 16.4 %copy-start = (s32[256,128]{1,0:T(8,128)S(1)}, s32[256,128]{1,0:T(8,128)}, u32[]{:S(2)}) copy-start(s32[256,128]{1,0:T(8,128)} %param.17) | copy-start | bytes 393220
  6.5 131.5 %all-reduce.3.cloned.1.call-start = ((), (), s32[]{:S(2)}) async-start(), calls=%async_computation.3 | async-start | bytes 5242880 | tf_op jit(solution)/shard_map/psum | solution.py:64
  21.0 0.7 copy-start.12
  21.0 1.1 copy-start.2
  21.0 2.5 copy-start.13
  21.0 117.0 %copy-start.8 = (f32[2560]{0:T(1024)S(1)}, f32[2560]{0:T(1024)}, u32[]{:S(2)}) copy-start(f32[2560]{0:T(1024)} %param.12) | copy-start | bytes 30724
  24.9 157.7 %copy-start.9 = (s32[32]{0:T(128)}, s32[32]{0:T(128)S(1)}, u32[]{:S(2)}) copy-start(s32[32]{0:T(128)S(1)} %get-tuple-element.6) | copy-start | bytes 388
  160.5 22.8 %all-to-all-start = ((bf16[4,64,2560]{2,1,0:T(8,128)(2,1)}), bf16[4,64,2560]{2,1,0:T(8,128)(2,1)S(1)}, u32[]{:S(2)}, u32[]{:S(2)}) async-start(bf16[4,64,2560]{2,1,0:T(8,128)(2,1)} %bitcast.8), calls=%async_computation | async-start | bytes 2621440 | tf_op jit(solution)/shard_map/all_to_all | solution.py:69
  164.1 153.6 %reduce-scatter.3.cloned.1.call-start = ((), (), s32[]{:S(2)}) async-start(), calls=%async_computation.4 | async-start | bytes 2359296 | tf_op jit(solution)/shard_map/reduce_scatter | solution.py:148
  164.3 20.6 %copy-start.11 = (s32[1024]{0:T(1024)}, s32[1024]{0:T(1024)S(1)}, u32[]{:S(2)}) copy-start(s32[1024]{0:T(1024)S(1)} %pad_clamp_fusion.2) | copy-start | bytes 12292
  182.6 2.0 copy-start.15
  183.4 4.4 %copy-start.5 = (pred[32,128]{1,0:T(8,128)(4,1)}, pred[32,128]{1,0:T(8,128)(4,1)S(1)}, u32[]{:S(2)}) copy-start(pred[32,128]{1,0:T(8,128)(4,1)S(1)} %fusion.25) | copy-start | bytes 12292
  202.1 3.5 copy-start.4
  203.5 37.2 %copy-start.6 = (pred[32,128]{1,0:T(8,128)(4,1)S(1)}, pred[32,128]{1,0:T(8,128)(4,1)}, u32[]{:S(2)}) copy-start(pred[32,128]{1,0:T(8,128)(4,1)} %copy-done.5) | copy-start | bytes 12292
  240.7 6.1 %copy-start.7 = (f32[32,64]{1,0:T(8,128)S(1)}, f32[32,64]{1,0:T(8,128)}, u32[]{:S(2)}) copy-start(f32[32,64]{1,0:T(8,128)} %exponential_select_fusion) | copy-start | bytes 24580
  240.7 6.4 %copy-start.10 = (s32[32]{0:T(128)S(1)}, s32[32]{0:T(128)}, u32[]{:S(2)}) copy-start(s32[32]{0:T(128)} %copy-done.9) | copy-start | bytes 388
  249.6 1.6 copy-start.16
  249.6 2.9 copy-start.14
  251.1 36.6 %copy-start.3 = (bf16[8,8,8,128]{3,1,2,0:T(8,128)(2,1)S(1)}, bf16[8,8,8,128]{3,1,2,0:T(8,128)(2,1)}, u32[]{:S(2)}) copy-start(bf16[8,8,8,128]{3,1,2,0:T(8,128)(2,1)} %get-tuple-element.13) | copy-start | bytes 393220
  251.1 143.9 %reduce-scatter.5.cloned.1.call-start = ((), (), s32[]{:S(2)}) async-start(), calls=%async_computation.5 | async-start | bytes 1179648 | tf_op jit(solution)/shard_map/reduce_scatter | solution.py:164
  326.1 69.0 %copy-start.1 = (s32[256,128]{1,0:T(8,128)S(1)}, s32[256,128]{1,0:T(8,128)}, u32[]{:S(2)}) copy-start(s32[256,128]{1,0:T(8,128)} %param.17) | copy-start | bytes 393220
Sparse Core Ops, SparseCore 0:
  21.2 116.7 all-reduce.2
  251.2 66.3 reduce-scatter.2
  331.8 63.1 reduce-scatter.4
where the time goes:
time: 403 us; the launch traced here: 402 us
  waiting for transfers between devices  206 us (51%)
  blocking collectives  85 us (21%)
  local copies, waits for them, and re-layouts  43.9 us (11%)
  matrix products  26.3 us (7%)
  other arithmetic  22.2 us (6%)
  between operations  14.2 us (4%)
    psum x1, waiting for transfers between devices, shards(): summed = lax.psum(partial_sum, 'seq')  113 us
    reduce_scatter x1, waiting for transfers between devices, shards(): lax.psum_scatter(jnp.dot(by_request, w_out, preferred_element_type=jnp.fl...  63.4 us
    pmax x1, blocking collectives, shards(): peak_score = lax.pmax(jnp.maximum(local_max, new_score), 'seq')  35 us
    unnamed x1, blocking collectives  33.8 us
    reduce_scatter x1, waiting for transfers between devices, shards(): lax.psum_scatter(scaled_out, 'seq', scatter_dimension=1, tiled=True)  29.7 us
    unnamed x45, local copies, waits for them, and re-layouts  22.6 us
    convert_element_type x1, other arithmetic, shards(): rotate_heads(summed + b_qkv[None, :], positions, col_start, HD, turned)  11.8 us
    all_gather x1, blocking collectives, shards(): lax.all_gather(hidden, 'grp', axis=0, tiled=True)  8.97 us
  transfers between devices with their start and end apart: 4, of which 3 were waited for; matrix products, arithmetic and copies ran while one was open for 6% of the time, Pallas kernels for 0%

commit v1 on v0

--- a/solution.py
+++ b/solution.py
@@ -61,7 +61,7 @@
     placed_at = restore[None, :] == request_ids[:, None]
     served_order = jnp.sum(jnp.where(placed_at, request_ids[None, :], 0), axis=1)
     served_ids = lax.dynamic_slice_in_dim(served_order, grp_index * group_size, group_size, 0)
-    summed = lax.psum(partial_sum, "seq")
+    summed = lax.all_gather(partial_sum, "seq").sum(axis=0)
     fresh_rows = rotate_heads(summed + b_qkv[None, :], positions, col_start, HD, turned).astype(
         jnp.bfloat16
     )

time: 403 us -> 687 us (1.70)
  waiting for transfers between devices: 206 us -> 492 us
    all_gather x0 -> x1, waiting for transfers between devices: none -> 399 us  [shards(): summed = lax.all_gather(partial_sum, 'seq').sum(axis=0)]
    psum x1 -> x0, waiting for transfers between devices: 113 us -> none  [shards(): summed = lax.psum(partial_sum, 'seq')]
    reduce_sum x0 -> x1, other arithmetic: none -> 8.67 us  [shards(): summed = lax.all_gather(partial_sum, 'seq').sum(axis=0)]
    unnamed x45 -> x43, local copies, waits for them, and re-layouts: 22.6 us -> 20.8 us
  transfers between devices with their start and end apart: 4 -> 4, of which waited for: 3 -> 3; matrix products, arithmetic and copies ran while one was open for 6% -> 3% of each run, Pallas kernels for 0% -> 0%
where the time goes in v1:
time: 687 us
  waiting for transfers between devices  492 us (72%)
  blocking collectives  85.9 us (13%)
  local copies, waits for them, and re-layouts  37.6 us (5%)
  other arithmetic  26.9 us (4%)
  matrix products  26.4 us (4%)
  between operations  14.2 us (2%)
    all_gather x1, waiting for transfers between devices, shards(): summed = lax.all_gather(partial_sum, 'seq').sum(axis=0)  399 us
    reduce_scatter x1, waiting for transfers between devices, shards(): lax.psum_scatter(jnp.dot(by_request, w_out, preferred_element_type=jnp.fl...  63.4 us
    pmax x1, blocking collectives, shards(): peak_score = lax.pmax(jnp.maximum(local_max, new_score), 'seq')  36 us
    unnamed x1, blocking collectives  33.7 us
    reduce_scatter x1, waiting for transfers between devices, shards(): lax.psum_scatter(scaled_out, 'seq', scatter_dimension=1, tiled=True)  29.7 us
    unnamed x43, local copies, waits for them, and re-layouts  20.8 us
  transfers between devices with their start and end apart: 4, of which 3 were waited for; matrix products, arithmetic and copies ran while one was open for 3% of the time, Pallas kernels for 0%

profile of v1, /device:TPU:0, one launch (start us, length us, event | category | flops | bytes accessed | tf_op | source)
XLA Modules:
  0.0 686.8 jit_solution(3415436405656623338)
XLA Ops:
  6.5 9.0 %all_gather.12 = bf16[256,1024]{1,0:T(8,128)(2,1)S(1)} all-gather(bf16[64,1024]{1,0:T(8,128)(2,1)} %param.10), channel_id=1, replica_groups=mesh['seq'=8,'grp'=4] {'grp'}, dimensions={0}, use_global_device_ids=true | all-gather | bytes 655360 | tf_op jit(solution)/shard_map/all_gather | solution.py:54
  15.5 5.5 fusion.40
  21.1 0.6 copy-done.11
  22.1 0.8 gather_fusion
  22.9 0.6 gather_fusion.1
  23.7 0.6 compare_select_fusion
  24.4 0.6 select_reduce_fusion.2
  25.0 398.8 %all-gather.3.cloned.1.call-done = f32[2048,2560]{1,0:T(8,128)} async-done(((f32[256,2560]{1,0:T(8,128)}), f32[2048,2560]{1,0:T(8,128)}) %all-gather.3.cloned.1.call-update) | async-done | bytes 20971536 | tf_op jit(solution)/shard_map/all_gather | solution.py:64
  423.8 8.7 %reduce_sum.44 = f32[256,2560]{1,0:T(8,128)S(1)} reduce(f32[8,256,2560]{2,1,0:T(8,128)} %bitcast.99, f32[]{:T(128)} %constant.86.clone.1), dimensions={0}, to_apply=%region_4.5 | reduce | flops 4587520 | bytes 23592964 | tf_op jit(solution)/shard_map/reduce_sum | solution.py:64
  432.5 2.3 copy.46
  434.8 2.1 broadcast_add_fusion
  436.9 0.2 slice_negate_fusion
  437.4 2.1 copy.47
  439.5 11.8 %select_convert_fusion = bf16[256,2560]{1,0:T(8,128)(2,1)S(1)} fusion(f32[256,2560]{1,0:T(8,128)} %copy.47, f32[256,2560]{1,0:T(8,128)} %copy-done.3, f32[2560]{0:T(1024)S(1)} %multiply_exponential_fusion, f32[256]{0:T(256)S(1)} %bitcast.125, f32[256]{0:T(256)S(1)} %bitcast.126, f32[256]{0:T(256)S(1)} %bitcast.124, f32[2560]{0:T(1024)S(1)} %copy-done.8, ...), kind=kLoop, calls=%fused_computation.12 | loop fusion | flops 5898240 | bytes 6584832 | tf_op jit(solution)/shard_map/convert_element_type | solution.py:65
  451.3 2.5 gather_fusion.3
  453.8 3.5 all-to-all-start
  457.3 0.2 reduce-scatter.3.cloned.1.call-start
  457.6 0.7 gather_fusion.2
  458.3 8.8 %copy.68 = bf16[512,8,8,128]{3,2,1,0:T(8,128)(2,1)} copy(bf16[512,8,8,128]{3,1,2,0:T(8,128)(2,1)} %bitcast.102) | data formatting | bytes 16777216
  467.1 8.8 %copy.69 = bf16[512,8,8,128]{3,2,1,0:T(8,128)(2,1)} copy(bf16[512,8,8,128]{3,1,2,0:T(8,128)(2,1)} %bitcast.103) | data formatting | bytes 16777216
  476.0 1.0 copy.48
  477.1 0.2 copy.66
  477.3 0.3 slice_bitcast_fusion.1
  477.6 0.9 gather_fusion.4
  478.6 6.9 %select_reduce_fusion.1 = (f32[32,8,8]{2,1,0:T(8,128)S(1)}, f32[32,8,8,128]{3,2,1,0:T(8,128)S(1)}) fusion(pred[32,128]{1,0:T(8,128)(4,1)S(1)} %fusion.25, bf16[32,8,8,128]{3,2,1,0:T(8,128)(2,1)S(1)} %bitcast.111, bf16[32,128,8,128]{3,2,1,0:T(8,128)(2,1)} %bitcast.98), kind=kOutput, calls=%fused_computation.26 | convolution fusion | flops 67893248 | bytes 9973760 | tf_op jit(solution)/shard_map/pkgd,ptkd->pkgt/dot_general | solution.py:95
  485.7 0.4 select_reduce_fusion
  486.1 0.7 copy.56
  486.8 1.2 gather_fusion.5
  488.0 0.3 copy.72
  488.4 0.7 fusion.41
  489.2 36.0 %pmax.7 = f32[64,64]{0,1:T(8,128)S(1)} all-reduce(f32[64,64]{0,1:T(8,128)S(1)} %fusion.38), channel_id=1, replica_groups=mesh['seq'=8,'grp'=4] {'seq'}, use_global_device_ids=true, to_apply=%region_7.8 | all-reduce | flops 4096 | bytes 32768 | tf_op jit(solution)/shard_map/pmax | solution.py:142
  525.3 0.7 exponential_select_fusion
  526.0 6.1 fusion
  532.1 0.3 mul.108
  532.4 2.5 multiply_bitcast_fusion
  535.0 1.5 copy.96
  536.5 0.6 dynamic-slice
  537.8 0.7 fusion.11
  538.6 0.3 convolution_multiply_fusion
  538.9 33.7 %all-reduce = f32[64,64]{0,1:T(8,128)S(1)} all-reduce(f32[64,64]{0,1:T(8,128)S(1)} %convolution_multiply_fusion), channel_id=4, replica_groups=mesh['seq'=8,'grp'=4] {'seq'}, use_global_device_ids=true, to_apply=%region_10.11.clone | all-reduce | flops 4096 | bytes 32768
  572.9 0.3 broadcast_bitcast_fusion
  573.1 29.7 %reduce-scatter.3.cloned.1.call-done = f32[64,1024]{1,0:T(8,128)} async-done(((f32[64,8192]{1,0:T(8,128)}), f32[64,1024]{1,0:T(8,128)}) %reduce-scatter.3.cloned.1.call-update) | async-done | bytes 262160 | tf_op jit(solution)/shard_map/reduce_scatter | solution.py:148
  602.8 1.0 copy.73
  603.8 0.2 fusion.18
  604.1 7.2 %all_gather.15 = bf16[256,1024]{1,0:T(8,128)(2,1)S(1)} all-gather(bf16[64,1024]{1,0:T(8,128)(2,1)S(1)} %bitcast.115), channel_id=1, replica_groups=mesh['seq'=8,'grp'=4] {'grp'}, dimensions={0}, use_global_device_ids=true | all-gather | bytes 655360 | tf_op jit(solution)/shard_map/all_gather | solution.py:162
  611.2 1.2 gather_fusion.6
  612.4 4.4 convolution_convert_fusion
  616.9 63.4 %reduce-scatter.5.cloned.1.call-done = bf16[32,2048]{1,0:T(8,128)(2,1)} async-done(((bf16[256,2048]{1,0:T(8,128)(2,1)}), bf16[32,2048]{1,0:T(8,128)(2,1)}) %reduce-scatter.5.cloned.1.call-update) | async-done | bytes 131088 | tf_op jit(solution)/shard_map/reduce_scatter | solution.py:164
  (73 shorter events, 2.1 us)
Async XLA Ops:
  6.5 16.4 %copy-start = (s32[256,128]{1,0:T(8,128)S(1)}, s32[256,128]{1,0:T(8,128)}, u32[]{:S(2)}) copy-start(s32[256,128]{1,0:T(8,128)} %param.17) | copy-start | bytes 393220
  6.5 417.3 %all-gather.3.cloned.1.call-start = ((), (), s32[]{:S(2)}) async-start(), calls=%async_computation.5 | async-start | bytes 23592960 | tf_op jit(solution)/shard_map/all_gather | solution.py:64
  21.1 0.7 copy-start.11
  21.1 1.1 copy-start.2
  21.1 2.5 copy-start.8
  21.1 2.6 copy-start.12
  25.0 450.9 %copy-start.9 = (s32[32]{0:T(128)}, s32[32]{0:T(128)S(1)}, u32[]{:S(2)}) copy-start(s32[32]{0:T(128)S(1)} %get-tuple-element.6) | copy-start | bytes 388
  432.5 2.3 copy-start.3
  453.8 22.2 %all-to-all-start = ((bf16[4,64,2560]{2,1,0:T(8,128)(2,1)}), bf16[4,64,2560]{2,1,0:T(8,128)(2,1)S(1)}, u32[]{:S(2)}, u32[]{:S(2)}) async-start(bf16[4,64,2560]{2,1,0:T(8,128)(2,1)} %bitcast.9), calls=%async_computation | async-start | bytes 2621440 | tf_op jit(solution)/shard_map/all_to_all | solution.py:69
  457.3 145.5 %reduce-scatter.3.cloned.1.call-start = ((), (), s32[]{:S(2)}) async-start(), calls=%async_computation.3 | async-start | bytes 2359296 | tf_op jit(solution)/shard_map/reduce_scatter | solution.py:148
  475.9 1.4 copy-start.14
  476.0 2.6 copy-start.5
  488.2 0.9 copy-start.4
  488.3 37.0 %copy-start.7 = (f32[32,64]{1,0:T(8,128)S(1)}, f32[32,64]{1,0:T(8,128)}, u32[]{:S(2)}) copy-start(f32[32,64]{1,0:T(8,128)} %gather_fusion.5) | copy-start | bytes 24580
  526.0 6.4 copy-start.10
  535.0 1.6 copy-start.15
  535.0 2.8 copy-start.13
  535.0 2.8 copy-start.6
  536.5 143.8 %reduce-scatter.5.cloned.1.call-start = ((), (), s32[]{:S(2)}) async-start(), calls=%async_computation.4 | async-start | bytes 1179648 | tf_op jit(solution)/shard_map/reduce_scatter | solution.py:164
  611.2 69.0 %copy-start.1 = (s32[256,128]{1,0:T(8,128)S(1)}, s32[256,128]{1,0:T(8,128)}, u32[]{:S(2)}) copy-start(s32[256,128]{1,0:T(8,128)} %param.17) | copy-start | bytes 393220
Sparse Core Ops, SparseCore 0:
  21.2 402.5 all-gather.2
  536.6 66.1 reduce-scatter.2
  617.0 63.2 reduce-scatter.4
